TPU v7x, 256 devices: a 2x2x32 block of a 4x8x32 slice. The times are simulated.
256 devices in a mesh: groups: 4 (over y, x), tp: 32 (over z), sp: 2 (over core).
Axes of the slice: x: 2, y: 2, z: 32, core: 2. Of those that a mesh axis runs over, the one named last changes fastest.
The devices are a block of a 4x8x32 slice.
Arguments:
- tokens: bfloat16 [12288, 4608], P(('groups', 'tp', 'sp')), parts along dimension 0, may hold values from -48 to 48
- w_query: bfloat16 [4608, 4096], P(None, 'tp'), may hold values from -0.09375 to 0.09375
- w_key: bfloat16 [4608, 2048], P(None, 'tp'), may hold values from -0.09375 to 0.09375
- w_value: bfloat16 [4608, 2048], P(None, 'tp'), may hold values from -0.09375 to 0.09375
- w_out: bfloat16 [4096, 4608], P('tp'), may hold values from -0.5 to 0.5
- doc_lengths: int32 [32], P('groups'), parts along dimension 0, may hold values from 1 to 768, 3072 in all
Outputs:
- attn_out: bfloat16 [12288, 4608], P(('groups', 'tp', 'sp')), parts along dimension 0
There are 4 independent parts, one for each index of `groups`. A program takes and returns all parts, laid end to end along the dimension named above; an argument that names none is the same for every part. Nothing has to cross between parts.
Inputs may be any that keep to these rules, and one draw needn't show every extreme that they name: `doc_lengths`: positive lengths that sum to 3072; the largest is exactly a quarter of 3072.
All inputs are finite; a program needn't handle non-finite values.
Results may differ from a plain program's by a relative error of at most 0.024.
Values may be sent and summed in bfloat16 or wider, within the bound.
A program may use at most 128 MiB of HBM per device.

v0:
```python
import jax
import jax.numpy as jnp
from jax import lax
from jax.sharding import PartitionSpec as P

PRE_SCALE = 144
masked_low = -1e30


def partner_2(block, axis, bit):
    count = lax.axis_size(axis)
    route = []
    for low in range(count):
        high = low | 1 << bit
        if high != low and high < count:
            route += [(low, high), (high, low)]
    return lax.ppermute(block, axis, route)


def rotate(matrix, places):
    half_width = matrix.shape[1] // 2
    spread = jnp.power(
        10000.0, -(jnp.arange(half_width, dtype=jnp.float32) * (2.0 / matrix.shape[1]))
    )
    angles = places.astype(jnp.float32)[:, None] * spread[None, :]
    cosine = jnp.cos(angles)
    sine_part = jnp.sin(angles)
    lower_part = matrix[:, :half_width]
    upper_part = matrix[:, half_width:]
    return jnp.concatenate(
        [
            lower_part * cosine - upper_part * sine_part,
            upper_part * cosine + lower_part * sine_part,
        ],
        axis=1,
    )


def doc_index(places, doc_ends):
    return jnp.sum((places[:, None] >= doc_ends[None, :]).astype(jnp.int32), axis=1)


def attend(running, queries, query_places, query_docs, key_rows, value_rows, key_places, key_docs):
    query_count = queries.shape[0]
    key_count = key_rows.shape[0]
    query_block = 512
    key_block = 512
    across = key_count // key_block

    def visit_tile(step_index, carried):
        query_start = step_index // across * query_block
        key_start = step_index % across * key_block
        query_part = lax.dynamic_slice_in_dim(queries, query_start, query_block, 0)
        place_part = lax.dynamic_slice_in_dim(query_places, query_start, query_block, 0)
        docs_part = lax.dynamic_slice_in_dim(query_docs, query_start, query_block, 0)
        key_part = lax.dynamic_slice_in_dim(key_rows, key_start, key_block, 0)
        value_part = lax.dynamic_slice_in_dim(value_rows, key_start, key_block, 0)
        key_place_part = lax.dynamic_slice_in_dim(key_places, key_start, key_block, 0)
        key_docs_part = lax.dynamic_slice_in_dim(key_docs, key_start, key_block, 0)
        largest_all, denominator_all, accum_all = carried
        largest_old = lax.dynamic_slice_in_dim(largest_all, query_start, query_block, 0)
        denominator_old = lax.dynamic_slice_in_dim(denominator_all, query_start, query_block, 0)
        accum_old = lax.dynamic_slice_in_dim(accum_all, query_start, query_block, 0)
        scores = jnp.einsum("qd,kd->qk", query_part, key_part, preferred_element_type=jnp.float32)
        allowed = (key_place_part[None, :] <= place_part[:, None]) & (
            key_docs_part[None, :] == docs_part[:, None]
        )
        largest_new = jnp.maximum(
            largest_old, jnp.max(jnp.where(allowed, scores, masked_low), axis=1, keepdims=True)
        )
        weights = jnp.where(allowed, jnp.exp(scores - largest_new), 0.0)
        fading = jnp.exp(largest_old - largest_new)
        denominator_new = denominator_old * fading + jnp.sum(weights, axis=1, keepdims=True)
        accum_new = accum_old * fading + jnp.dot(
            weights.astype(jnp.bfloat16), value_part, preferred_element_type=jnp.float32
        )
        return (
            lax.dynamic_update_slice_in_dim(largest_all, largest_new, query_start, 0),
            lax.dynamic_update_slice_in_dim(denominator_all, denominator_new, query_start, 0),
            lax.dynamic_update_slice_in_dim(accum_all, accum_new, query_start, 0),
        )

    return lax.fori_loop(0, query_count // query_block * across, visit_tile, running)


def pair_up(halves, places, tp_place, half_dim):
    partner = partner_2(halves, "tp", 0)
    is_even = tp_place % 2 == 0
    lower_rows = jnp.where(is_even, halves, partner)
    upper_rows = jnp.where(is_even, partner, halves)
    key_raw = jnp.concatenate([lower_rows[:, :half_dim], upper_rows[:, :half_dim]], axis=1)
    value_rows = jnp.concatenate([lower_rows[:, half_dim:], upper_rows[:, half_dim:]], axis=1)
    key_rows = rotate(key_raw.astype(jnp.float32), places).astype(jnp.bfloat16)
    return (key_rows, value_rows)


def local(tokens, w_query, w_key, w_value, w_out, doc_lengths):
    local_rows = tokens.shape[0]
    tp_count = lax.axis_size("tp")
    sp_count = lax.axis_size("sp")
    sp_place = lax.axis_index("sp")
    tp_place = lax.axis_index("tp")
    head_dim = w_query.shape[1]
    half_dim = w_key.shape[1]
    own_rows = local_rows * tp_count
    w_input = jnp.concatenate([w_query, w_key, w_value], axis=1)
    doc_ends = jnp.cumsum(doc_lengths)
    row_ids = jnp.arange(own_rows, dtype=jnp.int32)
    query_places = (row_ids // local_rows * sp_count + sp_place) * local_rows + row_ids % local_rows
    query_docs = doc_index(query_places, doc_ends)
    produced = jnp.dot(
        lax.all_gather(tokens, "tp", axis=0, tiled=True),
        w_input,
        preferred_element_type=jnp.float32,
    )
    query_raw = produced[:, :head_dim]
    halves = produced[:, head_dim:].astype(jnp.bfloat16)
    queries = (rotate(query_raw, query_places) * PRE_SCALE ** (-0.5)).astype(jnp.bfloat16)
    key_rows, value_rows = pair_up(halves, query_places, tp_place, half_dim)
    initial = (
        jnp.full((own_rows, 1), masked_low, jnp.float32),
        jnp.zeros((own_rows, 1), jnp.float32),
        jnp.zeros((own_rows, head_dim), jnp.float32),
    )
    shard_part = (
        lax.all_gather(key_rows, "sp", axis=0, tiled=True),
        lax.all_gather(value_rows, "sp", axis=0, tiled=True),
    )
    gathered_ids = jnp.arange(shard_part[0].shape[0], dtype=jnp.int32)
    source = gathered_ids // own_rows
    within = gathered_ids % own_rows
    places = (within // local_rows * sp_count + source) * local_rows + within % local_rows
    finished = attend(
        initial,
        queries,
        query_places,
        query_docs,
        shard_part[0],
        shard_part[1],
        places,
        doc_index(places, doc_ends),
    )
    largest_all, denominator_all, accum_all = finished
    attended = (accum_all / denominator_all).astype(jnp.bfloat16)
    return lax.psum_scatter(
        jnp.dot(attended, w_out, preferred_element_type=jnp.float32).astype(jnp.bfloat16),
        "tp",
        scatter_dimension=0,
        tiled=True,
    )


def solution(mesh):
    placed = (
        P(("groups", "tp", "sp"), None),
        P(None, "tp"),
        P(None, "tp"),
        P(None, "tp"),
        P("tp", None),
        P("groups"),
    )
    return jax.shard_map(
        local,
        mesh=mesh,
        in_specs=placed,
        out_specs=P(("groups", "tp", "sp"), None),
        check_vma=False,
    )
```

profile of v0, /device:TPU:37, one launch (start us, length us, event | category | flops | bytes accessed | tf_op | source)
XLA Modules:
  0.0 510.9 jit_solution(526202389130017574)
XLA Ops:
  7.4 2.3 copy.12
  9.7 1.4 copy.13
  11.1 185.4 %all-gather.2.cloned.1.call-done = bf16[1536,4608]{1,0:T(8,128)(2,1)} async-done(((bf16[48,4608]{1,0:T(8,128)(2,1)}), bf16[1536,4608]{1,0:T(8,128)(2,1)}) %all-gather.2.cloned.1.call-update) | async-done | bytes 14155792 | tf_op jit(solution)/shard_map/all_gather | solution.py:112
  196.5 9.7 %convolution_bitcast_fusion = f32[1536,256]{0,1:T(8,128)S(1)} fusion(bf16[1536,4608]{1,0:T(8,128)(2,1)} %all-gather.2.cloned.1.call-done, bf16[4608,64]{1,0:T(8,128)(2,1)} %copy.13, bf16[4608,64]{1,0:T(8,128)(2,1)} %copy.12, bf16[4608,128]{1,0:T(8,128)(2,1)} %param.9), kind=kOutput, calls=%fused_computation.29 | convolution fusion | flops 3630956544 | bytes 18087936 | tf_op jit(solution)/shard_map/dot_general | solution.py:111
  207.0 1.3 reduce-window.8
  208.4 1.3 convert_reduce_fusion.1
  209.7 1.4 convert_reduce_fusion
  211.1 4.7 collective-permute-done
  216.0 4.2 all_gather.11
  220.3 1.7 fusion.37
  222.0 2.4 all_gather.10
  224.5 0.8 fusion.25
  225.9 96.6 %while.19 = (s32[]{:T(128)}, f32[1536,1]{0,1:T(1,128)S(1)}, f32[1536,1]{0,1:T(1,128)}, f32[1536,128]{1,0:T(8,128)S(1)}, s32[3072]{0:T(1024)}, /*index=5*/s32[153...) while((s32[]{:T(128)}, f32[1536,1]{0,1:T(1,128)S(1)}, ...), condition=%wide.region_6.7_spmd, body=%wide.region_3.6_spmd.sunk | while | flops 138806304 | bytes 4209108 | solution.py:83
  227.4 0.8 dynamic_slice.139
  228.9 1.3 select_reduce_fusion.2
  232.8 0.8 dynamic_slice.139
  234.3 1.3 select_reduce_fusion.2
  238.1 0.8 dynamic_slice.139
  239.7 1.3 select_reduce_fusion.2
  243.5 0.8 dynamic_slice.139
  245.0 1.3 select_reduce_fusion.2
  248.9 0.8 dynamic_slice.139
  250.4 1.3 select_reduce_fusion.2
  254.3 0.8 dynamic_slice.139
  255.8 1.3 select_reduce_fusion.2
  261.2 1.3 select_reduce_fusion.2
  265.0 0.8 dynamic_slice.139
  266.5 1.3 select_reduce_fusion.2
  271.9 1.3 select_reduce_fusion.2
  275.8 0.8 dynamic_slice.139
  277.3 1.3 select_reduce_fusion.2
  282.7 1.3 select_reduce_fusion.2
  286.5 0.8 dynamic_slice.139
  288.0 1.3 select_reduce_fusion.2
  291.9 0.8 dynamic_slice.139
  293.4 1.3 select_reduce_fusion.2
  297.2 0.8 dynamic_slice.139
  298.8 1.3 select_reduce_fusion.2
  302.6 0.8 dynamic_slice.139
  304.1 1.3 select_reduce_fusion.2
  308.0 0.8 dynamic_slice.139
  309.5 1.3 select_reduce_fusion.2
  313.4 0.8 dynamic_slice.139
  314.9 1.3 select_reduce_fusion.2
  318.7 0.8 dynamic_slice.139
  320.3 1.3 select_reduce_fusion.2
  323.3 7.4 %convolution_convert_fusion = bf16[1536,4608]{1,0:T(8,128)(2,1)} fusion(bf16[128,4608]{1,0:T(8,128)(2,1)S(1)} %copy-done, f32[1536,128]{1,0:T(8,128)S(1)} %get-tuple-element.273, f32[1536]{0:T(1024)S(1)} %reduce), kind=kOutput, calls=%fused_computation.28 | convolution fusion | flops 1819410432 | bytes 16128000 | tf_op jit(solution)/shard_map/dot_general | solution.py:146
  330.8 173.2 %reduce-scatter.2.cloned.1.call-done = bf16[48,4608]{1,0:T(8,128)(2,1)} async-done(((bf16[1536,4608]{1,0:T(8,128)(2,1)}), bf16[48,4608]{1,0:T(8,128)(2,1)}) %reduce-scatter.2.cloned.1.call-update) | async-done | bytes 442384 | tf_op jit(solution)/shard_map/reduce_scatter | solution.py:145
  (266 shorter events, 63.4 us)
Async XLA Ops:
  6.5 316.8 %copy-start = (bf16[128,4608]{1,0:T(8,128)(2,1)S(1)}, bf16[128,4608]{1,0:T(8,128)(2,1)}, u32[]{:S(2)}) copy-start(bf16[128,4608]{1,0:T(8,128)(2,1)} %param.12) | copy-start | bytes 3538948
  6.6 3.1 copy-start.1
  6.6 190.0 %all-gather.2.cloned.1.call-start = ((), (), s32[]{:S(2)}) async-start(), calls=%async_computation.1 | async-start | bytes 14598144 | tf_op jit(solution)/shard_map/all_gather | solution.py:112
  7.3 496.7 %reduce-scatter.2.cloned.1.call-start = ((), (), s32[]{:S(2)}) async-start(), calls=%async_computation.2 | async-start | bytes 14598144 | tf_op jit(solution)/shard_map/reduce_scatter | solution.py:145
  11.1 197.2 %copy-start.3 = (s32[1536]{0:T(1024)}, s32[1536]{0:T(1024)S(1)}, u32[]{:S(2)}) copy-start(s32[1536]{0:T(1024)S(1)} %fusion.69) | copy-start | bytes 18436
  206.3 9.5 %collective-permute-start = (bf16[1536,128]{0,1:T(8,128)(2,1)S(1)}, bf16[1536,128]{0,1:T(8,128)(2,1)S(1)}, u32[]{:S(2)}, u32[]{:S(2)}) collective-permute-start(bf16[1536,128]{0,1:T(8,128)(2,1)S(1)} %slice.58), channel_id=1, source_target_pairs={{0,2},{2,0},{4,6},{6,4},{8,10},{10,8},{12,14},{14,12},{16,18},{18,... | collective-permute-start | bytes 1179656 | tf_op jit(solution)/shard_map/ppermute | solution.py:17
  208.4 2.7 copy-start.2
  215.9 4.4 copy-start.6
  227.4 3.2 copy-start.4
  230.6 0.6 copy-start.5
  232.8 3.2 copy-start.4
  236.0 0.6 copy-start.5
  238.1 3.2 copy-start.4
  241.4 0.6 copy-start.5
  243.5 3.2 copy-start.4
  246.7 0.6 copy-start.5
  248.9 3.2 copy-start.4
  252.1 0.6 copy-start.5
  254.3 3.2 copy-start.4
  257.5 0.6 copy-start.5
  259.6 3.2 copy-start.4
  262.9 0.6 copy-start.5
  265.0 3.2 copy-start.4
  268.2 0.6 copy-start.5
  270.4 3.2 copy-start.4
  273.6 0.6 copy-start.5
  275.7 3.2 copy-start.4
  279.0 0.6 copy-start.5
  281.1 3.2 copy-start.4
  284.3 0.6 copy-start.5
  286.5 3.2 copy-start.4
  289.7 0.6 copy-start.5
  291.9 3.2 copy-start.4
  295.1 0.6 copy-start.5
  297.2 3.2 copy-start.4
  300.5 0.6 copy-start.5
  302.6 3.2 copy-start.4
  305.8 0.6 copy-start.5
  308.0 3.2 copy-start.4
  311.2 0.6 copy-start.5
  313.4 3.2 copy-start.4
  316.6 0.6 copy-start.5
  318.7 3.2 copy-start.4
  322.0 0.6 copy-start.5
Sparse Core Ops, SparseCore 0:
  9.2 187.3 all-gather.1
  330.9 173.0 reduce-scatter.1
where the time goes:
time: 514 us; the launch traced here: 511 us
  waiting for transfers between devices  364 us (71%)
  local copies, waits for them, and re-layouts  59 us (11%)
  matrix products  51 us (10%)
  other arithmetic  14.6 us (3%)
  between operations  13.6 us (3%)
  blocking collectives  6.61 us (1%)
    all_gather x1, waiting for transfers between devices, local(): lax.all_gather(tokens, 'tp', axis=0, tiled=True)  185 us
    reduce_scatter x1, waiting for transfers between devices, local(): lax.psum_scatter(jnp.dot(attended, w_out, preferred_element_type=jnp.floa...  173 us
    dot_general x18, matrix products, visit_tile(): jnp.einsum('qd,kd->qk', query_part, key_part, preferred_element_type=jnp....  23.4 us
    dynamic_slice x18, local copies, waits for them, and re-layouts, visit_tile(): lax.dynamic_slice_in_dim(query_docs, query_start, query_block, 0)  13.8 us
    dynamic_slice x18, local copies, waits for them, and re-layouts, visit_tile(): key_docs_part = lax.dynamic_slice_in_dim(key_docs, key_start, key_block, 0)  13.6 us
    dynamic_slice x18, local copies, waits for them, and re-layouts, visit_tile(): lax.dynamic_slice_in_dim(query_places, query_start, query_block, 0)  13.5 us
    dynamic_slice x18, local copies, waits for them, and re-layouts, visit_tile(): lax.dynamic_slice_in_dim(key_places, key_start, key_block, 0)  13.5 us
    dot_general x18, matrix products, visit_tile(): jnp.dot(weights.astype(jnp.bfloat16), value_part, preferred_element_type=...  10.5 us
  transfers between devices with their start and end apart: 3, of which 3 were waited for; matrix products, arithmetic and copies ran while one was open for 2% of the time, Pallas kernels for 0%

commit v1 on v0

--- a/solution.py
+++ b/solution.py
@@ -5,6 +5,11 @@
 
 PRE_SCALE = 144
 masked_low = -1e30
+
+
+def gather_from_all(value, axis, dim):
+    copies = jnp.concatenate([value] * lax.axis_size(axis), axis=dim)
+    return lax.all_to_all(copies, axis, dim, dim, tiled=True)
 
 
 def partner_2(block, axis, bit):
@@ -109,9 +114,7 @@
     query_places = (row_ids // local_rows * sp_count + sp_place) * local_rows + row_ids % local_rows
     query_docs = doc_index(query_places, doc_ends)
     produced = jnp.dot(
-        lax.all_gather(tokens, "tp", axis=0, tiled=True),
-        w_input,
-        preferred_element_type=jnp.float32,
+        gather_from_all(tokens, "tp", 0), w_input, preferred_element_type=jnp.float32
     )
     query_raw = produced[:, :head_dim]
     halves = produced[:, head_dim:].astype(jnp.bfloat16)

time: 514 us -> 1620 us (3.15)
  waiting for transfers between devices: 364 us -> 1370 us
  starting transfers between devices: 0.21 us -> 51.4 us
  other arithmetic: 14.6 us -> 37.8 us
  local copies, waits for them, and re-layouts: 59 us -> 80.2 us
    all_to_all x0 -> x1, waiting for transfers between devices: none -> 1190 us  [gather_from_all(): return lax.all_to_all(copies, axis, dim, dim, tiled=True)]
    all_gather x1 -> x0, waiting for transfers between devices: 185 us -> none  [local(): lax.all_gather(tokens, 'tp', axis=0, tiled=True)]
    all_to_all x0 -> x1, starting transfers between devices: none -> 33.3 us  [gather_from_all(): return lax.all_to_all(copies, axis, dim, dim, tiled=True)]
    dynamic_update_slice x18, other arithmetic: 0.45 us -> 22.9 us  [visit_tile(): lax.dynamic_update_slice_in_dim(denominator_all, denominator_new, query_s...]
    unnamed x12 -> x47, local copies, waits for them, and re-layouts: 3.72 us -> 25.2 us
    ppermute x1, starting transfers between devices: 0.14 us -> 18 us  [partner_2(): return lax.ppermute(block, axis, route)]
  transfers between devices with their start and end apart: 3 -> 3, of which waited for: 3 -> 3; matrix products, arithmetic and copies ran while one was open for 2% -> 0% of each run, Pallas kernels for 0% -> 0%
where the time goes in v1:
time: 1620 us
  waiting for transfers between devices  1370 us (85%)
  local copies, waits for them, and re-layouts  80.2 us (5%)
  starting transfers between devices  51.4 us (3%)
  matrix products  50.5 us (3%)
  other arithmetic  37.8 us (2%)
    all_to_all x1, waiting for transfers between devices, gather_from_all(): return lax.all_to_all(copies, axis, dim, dim, tiled=True)  1190 us
    reduce_scatter x1, waiting for transfers between devices, local(): lax.psum_scatter(jnp.dot(attended, w_out, preferred_element_type=jnp.floa...  178 us
    all_to_all x1, starting transfers between devices, gather_from_all(): return lax.all_to_all(copies, axis, dim, dim, tiled=True)  33.3 us
  transfers between devices with their start and end apart: 3, of which 3 were waited for; matrix products, arithmetic and copies ran while one was open for 0% of the time, Pallas kernels for 0%

profile of v1, /device:TPU:37, one launch (start us, length us, event | category | flops | bytes accessed | tf_op | source)
XLA Modules:
  0.0 1617.1 jit_solution(7821138589711460142)
XLA Ops:
  24.1 5.1 copy-done.2
  29.2 33.3 %all-to-all-start = ((bf16[32,48,4608]{2,1,0:T(8,128)(2,1)}), bf16[32,48,4608]{2,1,0:T(8,128)(2,1)}, u32[]{:S(2)}, u32[]{:S(2)}) async-start(bf16[32,48,4608]{2,1,0:T(8,128)(2,1)} %bitcast.18), calls=%async_computation | async-start | bytes 28311552 | tf_op jit(solution)/shard_map/all_to_all | solution.py:12
  62.6 1.4 copy.12
  64.1 1.4 copy.13
  65.5 1190.9 %all-to-all-done = bf16[32,48,4608]{2,1,0:T(8,128)(2,1)} async-done(((bf16[32,48,4608]{2,1,0:T(8,128)(2,1)}), bf16[32,48,4608]{2,1,0:T(8,128)(2,1)}, u32[]{:S(2)}, u32[]{:S(2)}) %all-to-all-start) | async-done | bytes 14155808 | tf_op jit(solution)/shard_map/all_to_all | solution.py:12
  1256.4 9.7 fusion.20
  1266.2 18.0 %collective-permute-start = (bf16[1536,128]{0,1:T(8,128)(2,1)S(1)}, bf16[1536,128]{0,1:T(8,128)(2,1)S(1)}, u32[]{:S(2)}, u32[]{:S(2)}) collective-permute-start(bf16[1536,128]{0,1:T(8,128)(2,1)S(1)} %slice.58), channel_id=1, source_target_pairs={{0,2},{2,0},{4,6},{6,4},{8,10},{10,8},{12,14},{14,12},{16,18},{18,... | collective-permute-start | bytes 1179656 | tf_op jit(solution)/shard_map/ppermute | solution.py:22
  1284.8 1.3 reduce-window.8
  1286.2 1.3 convert_reduce_fusion.1
  1287.5 1.4 convert_reduce_fusion
  1290.1 9.6 all_gather.7
  1299.8 2.4 fusion.38
  1302.2 2.4 all_gather.6
  1306.1 117.7 %while.19 = (s32[]{:T(128)}, f32[1536,1]{0,1:T(1,128)S(1)}, f32[1536,1]{0,1:T(1,128)}, f32[1536,128]{1,0:T(8,128)S(1)}, s32[3072]{0:T(1024)}, /*index=5*/s32[153...) while((s32[]{:T(128)}, f32[1536,1]{0,1:T(1,128)S(1)}, ...), condition=%wide.region_6.7_spmd, body=%wide.region_3.6_spmd.sunk | while | flops 138806304 | bytes 4159900 | solution.py:88
  1309.1 1.3 select_reduce_fusion.2
  1310.8 1.3 constant_dynamic-update-slice_fusion.37
  1315.6 1.3 select_reduce_fusion.2
  1322.2 1.3 select_reduce_fusion.2
  1328.7 1.3 select_reduce_fusion.2
  1335.2 1.3 select_reduce_fusion.2
  1336.9 1.3 constant_dynamic-update-slice_fusion.37
  1341.7 1.3 select_reduce_fusion.2
  1348.3 1.3 select_reduce_fusion.2
  1349.9 1.3 constant_dynamic-update-slice_fusion.37
  1354.8 1.3 select_reduce_fusion.2
  1356.5 1.3 constant_dynamic-update-slice_fusion.37
  1361.4 1.3 select_reduce_fusion.2
  1363.0 1.3 constant_dynamic-update-slice_fusion.37
  1367.9 1.3 select_reduce_fusion.2
  1369.6 1.3 constant_dynamic-update-slice_fusion.37
  1374.5 1.3 select_reduce_fusion.2
  1376.1 1.3 constant_dynamic-update-slice_fusion.37
  1381.0 1.3 select_reduce_fusion.2
  1382.7 1.3 constant_dynamic-update-slice_fusion.37
  1387.6 1.3 select_reduce_fusion.2
  1389.2 1.3 constant_dynamic-update-slice_fusion.37
  1394.1 1.3 select_reduce_fusion.2
  1395.8 1.3 constant_dynamic-update-slice_fusion.37
  1400.7 1.3 select_reduce_fusion.2
  1402.3 1.3 constant_dynamic-update-slice_fusion.37
  1407.2 1.3 select_reduce_fusion.2
  1408.8 1.3 constant_dynamic-update-slice_fusion.37
  1413.7 1.3 select_reduce_fusion.2
  1415.4 1.3 constant_dynamic-update-slice_fusion.37
  1420.3 1.3 select_reduce_fusion.2
  1421.9 1.3 constant_dynamic-update-slice_fusion.37
  1424.5 7.4 convolution_convert_fusion
  1431.9 178.3 %reduce-scatter.2.cloned.1.call-done = bf16[48,4608]{1,0:T(8,128)(2,1)} async-done(((bf16[1536,4608]{1,0:T(8,128)(2,1)}), bf16[48,4608]{1,0:T(8,128)(2,1)}) %reduce-scatter.2.cloned.1.call-update) | async-done | bytes 442384 | tf_op jit(solution)/shard_map/reduce_scatter | solution.py:148
  (229 shorter events, 96.8 us)
Async XLA Ops:
  6.5 1417.9 %copy-start = (bf16[128,4608]{1,0:T(8,128)(2,1)S(1)}, bf16[128,4608]{1,0:T(8,128)(2,1)}, u32[]{:S(2)}) copy-start(bf16[128,4608]{1,0:T(8,128)(2,1)} %param.12) | copy-start | bytes 3538948
  6.6 16.9 %copy-start.1 = (bf16[48,4608]{1,0:T(8,128)(2,1)S(1)}, bf16[48,4608]{1,0:T(8,128)(2,1)}, u32[]{:S(2)}) copy-start(bf16[48,4608]{1,0:T(8,128)(2,1)} %param.8) | copy-start | bytes 1327108
  24.1 5.1 copy-start.2
  29.2 33.4 %copy-start.3 = (bf16[4608,64]{0,1:T(8,128)(2,1)S(1)}, bf16[4608,64]{0,1:T(8,128)(2,1)}, u32[]{:S(2)}) copy-start(bf16[4608,64]{0,1:T(8,128)(2,1)} %param.10) | copy-start | bytes 1769476
  29.2 34.8 %copy-start.4 = (bf16[4608,64]{0,1:T(8,128)(2,1)S(1)}, bf16[4608,64]{0,1:T(8,128)(2,1)}, u32[]{:S(2)}) copy-start(bf16[4608,64]{0,1:T(8,128)(2,1)} %param.11) | copy-start | bytes 1769476
  29.2 1227.2 %all-to-all-start = ((bf16[32,48,4608]{2,1,0:T(8,128)(2,1)}), bf16[32,48,4608]{2,1,0:T(8,128)(2,1)}, u32[]{:S(2)}, u32[]{:S(2)}) async-start(bf16[32,48,4608]{2,1,0:T(8,128)(2,1)} %bitcast.18), calls=%async_computation | async-start | bytes 28311552 | tf_op jit(solution)/shard_map/all_to_all | solution.py:12
  62.6 1547.7 %reduce-scatter.2.cloned.1.call-start = ((), (), s32[]{:S(2)}) async-start(), calls=%async_computation.2 | async-start | bytes 14598144 | tf_op jit(solution)/shard_map/reduce_scatter | solution.py:148
  65.5 1220.7 %copy-start.6 = (s32[1536]{0:T(1024)}, s32[1536]{0:T(1024)S(1)}, u32[]{:S(2)}) copy-start(s32[1536]{0:T(1024)S(1)} %fusion.70) | copy-start | bytes 18436
  1266.2 23.7 %collective-permute-start = (bf16[1536,128]{0,1:T(8,128)(2,1)S(1)}, bf16[1536,128]{0,1:T(8,128)(2,1)S(1)}, u32[]{:S(2)}, u32[]{:S(2)}) collective-permute-start(bf16[1536,128]{0,1:T(8,128)(2,1)S(1)} %slice.58), channel_id=1, source_target_pairs={{0,2},{2,0},{4,6},{6,4},{8,10},{10,8},{12,14},{14,12},{16,18},{18,... | collective-permute-start | bytes 1179656 | tf_op jit(solution)/shard_map/ppermute | solution.py:22
  1286.2 2.7 copy-start.5
Sparse Core Ops, SparseCore 0:
  1432.1 178.1 reduce-scatter.1
